TPU v7x, 128 devices: a whole 4x4x4 slice. The times are simulated.
128 devices in a mesh: row: 16 (over y, z), col: 8 (over x, core).
Axes of the slice: x: 4, y: 4, z: 4, core: 2. Of those that a mesh axis runs over, the one named last changes fastest.
Arguments:
- points: float32 [32768, 64], P(('col', 'row')), may hold values from -6 to 6
- feature_scale: float32 [64], replicated, may hold values from 0.1 to 0.5
- test_matrix: bfloat16 [32768, 256], P(('col', 'row')), may hold values from -6 to 6
- targets: float32 [32768], P(('col', 'row')), may hold values from -6 to 6
- ridge: float32 [1], replicated, may hold values from 0.5 to 2
Outputs:
- coefficients: float32 [32768], P(('col', 'row'))
- residual: float32 [32768], P(('col', 'row'))
- sketch: float32 [32768, 256], P(('col', 'row'))
All inputs are finite; a program needn't handle non-finite values.
Results may differ from a plain program's by a relative error of at most 0.012.
The roundings to bfloat16 on the way count: a program that leaves them out, or rounds other values in their place, can miss the bound.
Values may be sent and summed in bfloat16 or wider, within the bound.
No kernel may reach another device: no remote copies, remote signals or barrier semaphores. Data moves between devices by JAX's collectives and lax.ppermute only.
A program may use at most 128 MiB of HBM per device.

v0:
```python
import jax
import jax.numpy as jnp
from jax import lax
from jax.sharding import Mesh
from jax.sharding import PartitionSpec as P

ITERS = 2
ROW = ("row_0", "row_1")
COL = ("col_0", "col_1")
COL_ROW = ("col_0", "col_1", "row_0", "row_1")


def from_everyone(value, axis):
    devices = lax.axis_size(axis)
    return lax.all_to_all(
        jnp.broadcast_to(value[None], (devices, *value.shape)), axis, 0, 0, tiled=True
    )


def laid_out(pieces, dim):
    pieces = jnp.moveaxis(pieces, 0, dim)
    dims = pieces.shape
    return pieces.reshape(*dims[:dim], dims[dim] * dims[dim + 1], *dims[dim + 2 :])


def gathered_copies(value, axis, dim):
    pieces = from_everyone(value, axis)
    return laid_out(pieces, dim)


def in_blocks(value, dim, devices):
    before, after = (value.shape[:dim], value.shape[dim + 1 :])
    return jnp.moveaxis(value.reshape(*before, devices, -1, *after), dim, 0)


def sum_at_owner(value, axis, dim):
    devices = lax.axis_size(axis)
    pieces = lax.all_to_all(in_blocks(value, dim, devices), axis, 0, 0, tiled=True)
    return jnp.sum(pieces, axis=0)


def filled_up(lines, devices):
    spare = -len(lines) % devices
    return jnp.pad(lines, [(0, spare)] + [(0, 0)] * (lines.ndim - 1))


def gather_axes(value, axes, dim):
    far, near = axes
    pieces = from_everyone(from_everyone(value, far), near)
    return laid_out(pieces.swapaxes(0, 1).reshape(-1, *value.shape), dim)


def sum_in_two_steps(value, axes, dim):
    far, near = axes
    own = sum_at_owner(in_blocks(value, dim, lax.axis_size(far)), near, dim + 1)
    return jnp.sum(lax.all_to_all(own, far, 0, 0, tiled=True), axis=0)


def sum_by_parts(value, axes):
    lines = value.reshape(-1, value.shape[-1])
    padded = filled_up(lines, lax.axis_size(axes[0]) * lax.axis_size(axes[1]))
    whole = gather_axes(sum_in_two_steps(padded, axes, 0), axes, 0)
    return lax.slice_in_dim(whole, 0, len(lines)).reshape(value.shape)


def taken_together(value, axis):
    everything = from_everyone(value, axis)
    return jnp.sum(everything, axis=0)


def by_axis(value, axes):
    far, near = axes
    return taken_together(taken_together(value, near), far)


def packed_total(arrays, axis):
    flat, at, gathered = (jnp.concatenate([a.reshape(-1) for a in arrays]), 0, [])
    running = by_axis(flat, axis)
    for a in arrays:
        gathered.append(running[at : at + a.size].reshape(a.shape))
        at += a.size
    return tuple(gathered)


def kernel_block(left, left_norm, right, right_norm):
    cross = lax.dot_general(
        left,
        right,
        (((1,), (1,)), ((), ())),
        precision=lax.Precision.HIGHEST,
        preferred_element_type=jnp.float32,
    )
    return jnp.exp(-0.5 * (left_norm[:, None] + right_norm[None, :] - 2.0 * cross))


def squared(scaled):
    return jnp.sum(scaled * scaled, axis=1)


def sketch_term(left, left_norm, right, right_norm, test_block):
    weights = kernel_block(left, left_norm, right, right_norm).astype(jnp.bfloat16)
    return jnp.dot(weights, test_block, preferred_element_type=jnp.float32)


def core_solve(lower, vector):
    middle = lax.linalg.triangular_solve(lower, vector[:, None], left_side=True, lower=True)
    return lax.linalg.triangular_solve(lower, middle, left_side=True, lower=True, transpose_a=True)[
        :, 0
    ]


def local(points, feature_scale, test_matrix, targets, ridge):
    ridge_value = ridge[0]
    scaled = points * feature_scale[None, :]
    test_wide = test_matrix.astype(jnp.float32)
    column_pts = gathered_copies(scaled, ROW, 0)
    column_rows = gathered_copies(test_matrix, ROW, 0)
    row_pts = gathered_copies(scaled, COL, 0)
    row_norm = squared(row_pts)
    column_norm = squared(column_pts)
    sketch = sum_at_owner(
        sketch_term(row_pts, row_norm, column_pts, column_norm, column_rows), COL, 0
    )
    shifted = ridge_value * test_wide + sketch
    local_core = lax.dot_general(
        shifted,
        sketch,
        (((0,), (0,)), ((), ())),
        precision=lax.Precision.HIGHEST,
        preferred_element_type=jnp.float32,
    )
    core = sum_by_parts(local_core, (("row_0", "row_1", "col_0"), "col_1"))
    lower = jnp.linalg.cholesky(core)

    def operate(vector):
        column_vec = gathered_copies(vector, ROW, 0)
        weights = kernel_block(row_pts, row_norm, column_pts, column_norm)
        return (
            sum_at_owner(
                jnp.dot(
                    weights,
                    column_vec,
                    precision=lax.Precision.HIGHEST,
                    preferred_element_type=jnp.float32,
                ),
                COL,
                0,
            )
            + ridge_value * vector
        )

    def precondition(resid):
        local_proj = jnp.dot(
            resid, sketch, precision=lax.Precision.HIGHEST, preferred_element_type=jnp.float32
        )
        projected, square_sum = packed_total(
            (local_proj, jnp.sum(resid * resid)), (("row_0", "row_1", "col_0"), "col_1")
        )
        solved = core_solve(lower, projected)
        precond = (
            resid
            - jnp.dot(
                sketch, solved, precision=lax.Precision.HIGHEST, preferred_element_type=jnp.float32
            )
        ) / ridge_value
        descent = (square_sum - jnp.sum(projected * solved)) / ridge_value
        return (precond, descent)

    coefficients = jnp.zeros_like(targets)
    resid = targets
    precond, descent = precondition(resid)
    direction = precond
    for turn in range(ITERS):
        image = operate(direction)
        step_size = descent / by_axis(
            jnp.sum(direction * image), (("row_0", "row_1", "col_0"), "col_1")
        )
        coefficients = coefficients + step_size * direction
        if turn + 1 < ITERS:
            resid = resid - step_size * image
            precond, fresh = precondition(resid)
            direction = precond + fresh / descent * direction
            descent = fresh
    residual = targets - operate(coefficients)
    return (coefficients, residual, sketch)


def solution(mesh):
    split = Mesh(mesh.devices.reshape(4, 4, 4, 2), ("row_0", "row_1", "col_0", "col_1"))
    return jax.shard_map(
        local,
        mesh=split,
        in_specs=(P(COL_ROW, None), P(), P(COL_ROW, None), P(COL_ROW), P()),
        out_specs=(P(COL_ROW), P(COL_ROW), P(COL_ROW, None)),
        check_vma=False,
    )
```

profile of v0, /device:TPU:1, one launch (start us, length us, event | category | flops | bytes accessed | tf_op | source)
XLA Modules:
  0.0 479.9 jit_solution(10804222295952694651)
XLA Ops:
  1.6 14.9 %all_to_all.133 = f32[8,256,64]{1,2,0:T(8,128)S(1)} all-to-all(f32[8,256,64]{1,2,0:T(8,128)S(1)} %broadcast_in_dim.38), channel_id=1, replica_groups=mesh['row_0'=4,'row_1'=4,'col_0'=4,'col_1'=2] {'col_0','col_1'}, dimensions={0} | all-to-all | bytes 1048576 | tf_op jit(solution)/shard_map/all_to_all | solution.py:15
  17.6 7.8 %all-to-all-start.1 = ((f32[16,256,64]{1,2,0:T(8,128)}), f32[16,256,64]{1,2,0:T(8,128)S(1)}, u32[]{:S(2)}, u32[]{:S(2)}) async-start(f32[16,256,64]{1,2,0:T(8,128)} %broadcast_in_dim.39), calls=%async_computation.1 | async-start | bytes 2097152 | tf_op jit(solution)/shard_map/all_to_all | solution.py:15
  25.5 15.3 %all-to-all-done.1 = f32[16,256,64]{1,2,0:T(8,128)S(1)} async-done(((f32[16,256,64]{1,2,0:T(8,128)}), f32[16,256,64]{1,2,0:T(8,128)S(1)}, u32[]{:S(2)}, u32[]{:S(2)}) %all-to-all-start.1) | async-done | bytes 1048608 | tf_op jit(solution)/shard_map/all_to_all | solution.py:15
  48.0 37.6 %fusion.19 = (bf16[2048,4096]{1,0:T(8,128)(2,1)}, f32[2048,4096]{1,0:T(8,128)}) fusion(f32[2048,64]{0,1:T(8,128)S(1)} %bitcast.208, f32[4096,64]{0,1:T(8,128)S(1)} %bitcast.207, f32[4096]{0:T(1024)S(1)} %bitcast.210, f32[2048]{0:T(1024)S(1)} %bitcast.211), kind=kOutput, calls=%fused_computation.74 | convolution fusion | flops 6484393984 | bytes 51929088 | tf_op jit(solution)/shard_map/dot_general | solution.py:86
  85.6 12.4 %fusion.20 = f32[8,256,256]{2,1,0:T(8,128)} fusion(bf16[8,256,4096]{2,1,0:T(8,128)(2,1)} %bitcast.204, bf16[4096,256,1]{1,0,2:T(8,128)(2,1)} %bitcast.2), kind=kOutput, calls=%fused_computation.75 | convolution fusion | flops 4294967296 | bytes 20971520 | tf_op jit(solution)/shard_map/dot_general | solution.py:102
  98.0 6.6 %all-to-all-start.3 = ((f32[8,256,256]{2,1,0:T(8,128)}), f32[8,256,256]{2,1,0:T(8,128)S(1)}, u32[]{:S(2)}, u32[]{:S(2)}) async-start(f32[8,256,256]{2,1,0:T(8,128)} %fusion.20), calls=%async_computation.3 | async-start | bytes 4194304 | tf_op jit(solution)/shard_map/all_to_all | solution.py:38
  105.9 25.0 %all-to-all-done.3 = f32[8,256,256]{2,1,0:T(8,128)S(1)} async-done(((f32[8,256,256]{2,1,0:T(8,128)}), f32[8,256,256]{2,1,0:T(8,128)S(1)}, u32[]{:S(2)}, u32[]{:S(2)}) %all-to-all-start.3) | async-done | bytes 2097184 | tf_op jit(solution)/shard_map/all_to_all | solution.py:38
  141.7 8.3 %all-to-all-start.7 = ((f32[64,2,256]{2,1,0:T(2,128)}), f32[64,2,256]{2,1,0:T(2,128)S(1)}, u32[]{:S(2)}, u32[]{:S(2)}) async-start(f32[64,2,256]{2,1,0:T(2,128)} %copy.47), calls=%async_computation.7 | async-start | bytes 262144 | tf_op jit(solution)/shard_map/all_to_all | solution.py:56
  150.0 8.7 %all-to-all-done.7 = f32[64,2,256]{2,1,0:T(2,128)S(1)} async-done(((f32[64,2,256]{2,1,0:T(2,128)}), f32[64,2,256]{2,1,0:T(2,128)S(1)}, u32[]{:S(2)}, u32[]{:S(2)}) %all-to-all-start.7) | async-done | bytes 131104 | tf_op jit(solution)/shard_map/all_to_all | solution.py:56
  159.5 4.9 %all-to-all-start.5 = ((f32[64,1,257]{2,1,0:T(1,128)}), f32[64,1,257]{2,1,0:T(1,128)S(1)}, u32[]{:S(2)}, u32[]{:S(2)}) async-start(f32[64,1,257]{2,1,0:T(1,128)} %broadcast_in_dim.42), calls=%async_computation.5 | async-start | bytes 196608 | tf_op jit(solution)/shard_map/all_to_all | solution.py:15
  164.5 8.5 %all-to-all-done.5 = f32[64,1,257]{2,1,0:T(1,128)S(1)} async-done(((f32[64,1,257]{2,1,0:T(1,128)}), f32[64,1,257]{2,1,0:T(1,128)S(1)}, u32[]{:S(2)}, u32[]{:S(2)}) %all-to-all-start.5) | async-done | bytes 65824 | tf_op jit(solution)/shard_map/all_to_all | solution.py:15
  173.7 5.0 %all-to-all-start.8 = ((f32[64,2,256]{2,1,0:T(2,128)}), f32[64,2,256]{2,1,0:T(2,128)S(1)}, u32[]{:S(2)}, u32[]{:S(2)}) async-start(f32[64,2,256]{2,1,0:T(2,128)} %broadcast_in_dim.43), calls=%async_computation.8 | async-start | bytes 262144 | tf_op jit(solution)/shard_map/all_to_all | solution.py:15
  178.8 8.6 %all-to-all-done.8 = f32[64,2,256]{2,1,0:T(2,128)S(1)} async-done(((f32[64,2,256]{2,1,0:T(2,128)}), f32[64,2,256]{2,1,0:T(2,128)S(1)}, u32[]{:S(2)}, u32[]{:S(2)}) %all-to-all-start.8) | async-done | bytes 131104 | tf_op jit(solution)/shard_map/all_to_all | solution.py:15
  187.5 7.8 %all_to_all.136 = f32[2,64,2,256]{3,2,1,0:T(2,128)S(1)} all-to-all(f32[2,64,2,256]{3,2,1,0:T(2,128)S(1)} %broadcast_in_dim.44), channel_id=1, replica_groups=mesh['row_0'=4,'row_1'=4,'col_0'=4,'col_1'=2] {'col_1'}, dimensions={0} | all-to-all | bytes 524288 | tf_op jit(solution)/shard_map/all_to_all | solution.py:15
  195.7 11.7 %cholesky.50 = f32[128,128]{1,0:T(8,128)S(1)} custom-call(f32[128,128]{1,0:T(8,128)S(1)} %cholesky.118), custom_call_target="Cholesky" | custom-call | tf_op jit(solution)/shard_map/jit(cholesky)/cholesky | solution.py:133
  207.5 9.8 %custom-call.17 = f32[1,128,128]{1,2,0:T(8,128)S(1)} custom-call(f32[1,128,128]{2,1,0:T(8,128)S(1)} %get-tuple-element.52), custom_call_target="InvertDiagBlocksLowerTriangular" | custom-call | tf_op jit(solution)/shard_map/jit(cholesky)/cholesky | solution.py:133
  217.8 11.7 %cholesky.105 = f32[128,128]{1,0:T(8,128)S(1)} custom-call(f32[128,128]{1,0:T(8,128)S(1)} %convolution_subtract_fusion), custom_call_target="Cholesky" | custom-call | tf_op jit(solution)/shard_map/jit(cholesky)/cholesky | solution.py:133
  235.7 19.9 %custom-call.21 = f32[2,128,128]{1,2,0:T(8,128)S(1)} custom-call(f32[2,128,128]{2,1,0:T(8,128)S(1)} %get-tuple-element.34), custom_call_target="InvertDiagBlocksLowerTriangular" | custom-call | tf_op jit(solution)/shard_map/triangular_solve/custom-call.4 | solution.py:107
  261.8 5.9 %all-to-all-done.10 = f32[16,1,256]{2,1,0:T(1,128)S(1)} async-done(((f32[16,1,256]{2,1,0:T(1,128)}), f32[16,1,256]{2,1,0:T(1,128)S(1)}, u32[]{:S(2)}, u32[]{:S(2)}) %all-to-all-start.10) | async-done | bytes 16416 | tf_op jit(solution)/shard_map/all_to_all | solution.py:15
  267.7 31.7 %fusion.22 = f32[1,8,256]{2,0,1:T(1,128)S(1)} fusion(f32[8,256,4096]{2,1,0:T(8,128)} %bitcast.201, f32[4096,1,1]{0,1,2:T(1,128)S(1)} %bitcast.212), kind=kOutput, calls=%fused_computation.77 | convolution fusion | flops 100663296 | bytes 33579008 | tf_op jit(solution)/shard_map/dot_general | solution.py:140
  304.5 4.6 all-to-all-done.11
  322.9 6.5 %all-to-all-done.13 = f32[64,1,1]{2,1,0:T(1,128)S(1)} async-done(((f32[64,1,1]{2,1,0:T(1,128)}), f32[64,1,1]{2,1,0:T(1,128)S(1)}, u32[]{:S(2)}, u32[]{:S(2)}) %all-to-all-start.13) | async-done | bytes 288 | tf_op jit(solution)/shard_map/all_to_all | solution.py:15
  332.3 5.1 %all_to_all.138 = f32[2,1,257]{2,1,0:T(1,128)S(1)} all-to-all(f32[2,1,257]{2,1,0:T(1,128)S(1)} %broadcast_in_dim.49), channel_id=1, replica_groups=mesh['row_0'=4,'row_1'=4,'col_0'=4,'col_1'=2] {'col_1'}, dimensions={0} | all-to-all | bytes 4112 | tf_op jit(solution)/shard_map/all_to_all | solution.py:15
  338.1 5.0 %all-to-all-start.15 = ((f32[64,1,257]{2,1,0:T(1,128)}), f32[64,1,257]{2,1,0:T(1,128)S(1)}, u32[]{:S(2)}, u32[]{:S(2)}) async-start(f32[64,1,257]{2,1,0:T(1,128)} %broadcast_in_dim.50), calls=%async_computation.15 | async-start | bytes 196608 | tf_op jit(solution)/shard_map/all_to_all | solution.py:15
  343.1 8.6 %all-to-all-done.15 = f32[64,1,257]{2,1,0:T(1,128)S(1)} async-done(((f32[64,1,257]{2,1,0:T(1,128)}), f32[64,1,257]{2,1,0:T(1,128)S(1)}, u32[]{:S(2)}, u32[]{:S(2)}) %all-to-all-start.15) | async-done | bytes 65824 | tf_op jit(solution)/shard_map/all_to_all | solution.py:15
  355.8 9.7 %all_to_all.139 = f32[16,1,256]{2,1,0:T(1,128)S(1)} all-to-all(f32[16,1,256]{2,1,0:T(1,128)S(1)} %broadcast_in_dim.52), channel_id=1, replica_groups=mesh['row_0'=4,'row_1'=4,'col_0'=4,'col_1'=2] {'row_0','row_1'}, dimensions={0} | all-to-all | bytes 32768 | tf_op jit(solution)/shard_map/all_to_all | solution.py:15
  365.5 31.7 %fusion.24 = f32[1,8,256]{2,0,1:T(1,128)S(1)} fusion(f32[8,256,4096]{2,1,0:T(8,128)} %bitcast.202, f32[4096,1,1]{0,1,2:T(1,128)S(1)} %bitcast.215), kind=kOutput, calls=%fused_computation.79 | convolution fusion | flops 100663296 | bytes 33579008 | tf_op jit(solution)/shard_map/dot_general | solution.py:140
  397.2 9.9 %all_to_all.140 = f32[8,1,256]{2,1,0:T(1,128)S(1)} all-to-all(f32[8,1,256]{2,1,0:T(1,128)S(1)} %all_to_all.104), channel_id=1, replica_groups=mesh['row_0'=4,'row_1'=4,'col_0'=4,'col_1'=2] {'col_0','col_1'}, dimensions={0} | all-to-all | bytes 16384 | tf_op jit(solution)/shard_map/all_to_all | solution.py:38
  413.7 12.7 %all_to_all.142 = f32[64,1,1]{2,1,0:T(1,128)S(1)} all-to-all(f32[64,1,1]{2,1,0:T(1,128)S(1)} %broadcast_in_dim.54), channel_id=1, replica_groups=mesh['row_0'=4,'row_1'=4,'col_0'=4,'col_1'=2] {'row_0','row_1','col_0'}, dimensions={0} | all-to-all | bytes 512 | tf_op jit(solution)/shard_map/all_to_all | solution.py:15
  427.7 9.5 %all_to_all.143 = f32[16,1,256]{2,1,0:T(1,128)S(1)} all-to-all(f32[16,1,256]{2,1,0:T(1,128)S(1)} %broadcast_in_dim.55), channel_id=1, replica_groups=mesh['row_0'=4,'row_1'=4,'col_0'=4,'col_1'=2] {'row_0','row_1'}, dimensions={0} | all-to-all | bytes 32768 | tf_op jit(solution)/shard_map/all_to_all | solution.py:15
  437.3 31.7 %fusion.25 = f32[1,8,256]{2,0,1:T(1,128)S(1)} fusion(f32[8,256,4096]{2,1,0:T(8,128)} %bitcast.203, f32[4096,1,1]{0,1,2:T(1,128)S(1)} %bitcast.213), kind=kOutput, calls=%fused_computation.80 | convolution fusion | flops 100663296 | bytes 33579008 | tf_op jit(solution)/shard_map/dot_general | solution.py:140
  469.0 10.2 %all_to_all.144 = f32[8,1,256]{2,1,0:T(1,128)S(1)} all-to-all(f32[8,1,256]{2,1,0:T(1,128)S(1)} %all_to_all.109), channel_id=1, replica_groups=mesh['row_0'=4,'row_1'=4,'col_0'=4,'col_1'=2] {'col_0','col_1'}, dimensions={0} | all-to-all | bytes 16384 | tf_op jit(solution)/shard_map/all_to_all | solution.py:38
  (121 shorter events, 69.3 us)
Async XLA Ops:
  17.6 23.2 %all-to-all-start.1 = ((f32[16,256,64]{1,2,0:T(8,128)}), f32[16,256,64]{1,2,0:T(8,128)S(1)}, u32[]{:S(2)}, u32[]{:S(2)}) async-start(f32[16,256,64]{1,2,0:T(8,128)} %broadcast_in_dim.39), calls=%async_computation.1 | async-start | bytes 2097152 | tf_op jit(solution)/shard_map/all_to_all | solution.py:15
  43.3 42.3 %all-to-all-start.2 = ((bf16[16,256,256]{2,1,0:T(8,128)(2,1)}), bf16[16,256,256]{2,1,0:T(8,128)(2,1)}, u32[]{:S(2)}, u32[]{:S(2)}) async-start(bf16[16,256,256]{2,1,0:T(8,128)(2,1)} %broadcast_in_dim.40), calls=%async_computation.2 | async-start | bytes 4194304 | tf_op jit(solution)/shard_map/all_to_all | solution.py:15
  47.9 57.3 %copy-start.2 = (f32[256]{0:T(256)S(1)}, f32[256]{0:T(256)}, u32[]{:S(2)}) copy-start(f32[256]{0:T(256)} %param.12) | copy-start | bytes 3076
  47.9 83.1 %copy-start.1 = (bf16[256,256]{1,0:T(8,128)(2,1)S(1)}, bf16[256,256]{1,0:T(8,128)(2,1)}, u32[]{:S(2)}) copy-start(bf16[256,256]{1,0:T(8,128)(2,1)} %param.11) | copy-start | bytes 393220
  98.0 32.8 %all-to-all-start.3 = ((f32[8,256,256]{2,1,0:T(8,128)}), f32[8,256,256]{2,1,0:T(8,128)S(1)}, u32[]{:S(2)}, u32[]{:S(2)}) async-start(f32[8,256,256]{2,1,0:T(8,128)} %fusion.20), calls=%async_computation.3 | async-start | bytes 4194304 | tf_op jit(solution)/shard_map/all_to_all | solution.py:38
  131.0 266.1 %copy-start = (f32[256,256]{1,0:T(8,128)}, f32[256,256]{1,0:T(8,128)S(1)}, u32[]{:S(2)}) copy-start(f32[256,256]{1,0:T(8,128)S(1)} %reduce_sum.200) | copy-start | bytes 786436
  141.7 17.1 %all-to-all-start.7 = ((f32[64,2,256]{2,1,0:T(2,128)}), f32[64,2,256]{2,1,0:T(2,128)S(1)}, u32[]{:S(2)}, u32[]{:S(2)}) async-start(f32[64,2,256]{2,1,0:T(2,128)} %copy.47), calls=%async_computation.7 | async-start | bytes 262144 | tf_op jit(solution)/shard_map/all_to_all | solution.py:56
  159.5 13.6 %all-to-all-start.5 = ((f32[64,1,257]{2,1,0:T(1,128)}), f32[64,1,257]{2,1,0:T(1,128)S(1)}, u32[]{:S(2)}, u32[]{:S(2)}) async-start(f32[64,1,257]{2,1,0:T(1,128)} %broadcast_in_dim.42), calls=%async_computation.5 | async-start | bytes 196608 | tf_op jit(solution)/shard_map/all_to_all | solution.py:15
  173.7 13.7 %all-to-all-start.8 = ((f32[64,2,256]{2,1,0:T(2,128)}), f32[64,2,256]{2,1,0:T(2,128)S(1)}, u32[]{:S(2)}, u32[]{:S(2)}) async-start(f32[64,2,256]{2,1,0:T(2,128)} %broadcast_in_dim.43), calls=%async_computation.8 | async-start | bytes 262144 | tf_op jit(solution)/shard_map/all_to_all | solution.py:15
  257.8 9.9 %all-to-all-start.10 = ((f32[16,1,256]{2,1,0:T(1,128)}), f32[16,1,256]{2,1,0:T(1,128)S(1)}, u32[]{:S(2)}, u32[]{:S(2)}) async-start(f32[16,1,256]{2,1,0:T(1,128)} %broadcast_in_dim.46), calls=%async_computation.10 | async-start | bytes 32768 | tf_op jit(solution)/shard_map/all_to_all | solution.py:15
  299.9 9.2 %all-to-all-start.11 = ((f32[8,1,256]{2,1,0:T(1,128)}), f32[8,1,256]{2,1,0:T(1,128)S(1)}, u32[]{:S(2)}, u32[]{:S(2)}) async-start(f32[8,1,256]{2,1,0:T(1,128)} %all_to_all.97), calls=%async_computation.11 | async-start | bytes 16384 | tf_op jit(solution)/shard_map/all_to_all | solution.py:38
  316.3 13.0 %all-to-all-start.13 = ((f32[64,1,1]{2,1,0:T(1,128)}), f32[64,1,1]{2,1,0:T(1,128)S(1)}, u32[]{:S(2)}, u32[]{:S(2)}) async-start(f32[64,1,1]{2,1,0:T(1,128)} %broadcast_in_dim.48), calls=%async_computation.13 | async-start | bytes 65536 | tf_op jit(solution)/shard_map/all_to_all | solution.py:15
  338.1 13.6 %all-to-all-start.15 = ((f32[64,1,257]{2,1,0:T(1,128)}), f32[64,1,257]{2,1,0:T(1,128)S(1)}, u32[]{:S(2)}, u32[]{:S(2)}) async-start(f32[64,1,257]{2,1,0:T(1,128)} %broadcast_in_dim.50), calls=%async_computation.15 | async-start | bytes 196608 | tf_op jit(solution)/shard_map/all_to_all | solution.py:15
  427.7 52.0 %copy-start.3 = (f32[256]{0:T(256)}, f32[256]{0:T(256)S(1)}, u32[]{:S(2)}) copy-start(f32[256]{0:T(256)S(1)} %multiply_add_fusion) | copy-start | bytes 3076
where the time goes:
time: 488 us; the launch traced here: 480 us
  matrix products  149 us (31%)
  blocking collectives  96.1 us (20%)
  waiting for transfers between devices  91.8 us (19%)
  other arithmetic  63.9 us (13%)
  starting transfers between devices  54.7 us (11%)
  local copies, waits for them, and re-layouts  16.9 us (3%)
  between operations  7.37 us (2%)
    dot_general x3, matrix products, operate(): jnp.dot(weights, column_vec, precision=lax.Precision.HIGHEST, preferred_e...  95 us
    all_to_all x9, blocking collectives, from_everyone(): lax.all_to_all(jnp.broadcast_to(value[None], (devices, *value.shape)), ax...  71.5 us
    all_to_all x7, waiting for transfers between devices, from_everyone(): lax.all_to_all(jnp.broadcast_to(value[None], (devices, *value.shape)), ax...  53.5 us
    dot_general x1, matrix products, kernel_block(): lax.dot_general(left, right, (((1,), (1,)), ((), ())), precision=lax.Prec...  37.6 us
    all_to_all x7, starting transfers between devices, from_everyone(): lax.all_to_all(jnp.broadcast_to(value[None], (devices, *value.shape)), ax...  35.2 us
    another operation x6, other arithmetic, local(): lower = jnp.linalg.cholesky(core)  34 us
    all_to_all x2, waiting for transfers between devices, sum_at_owner(): lax.all_to_all(in_blocks(value, dim, devices), axis, 0, 0, tiled=True)  29.6 us
    all_to_all x3, blocking collectives, sum_at_owner(): lax.all_to_all(in_blocks(value, dim, devices), axis, 0, 0, tiled=True)  24.6 us
  transfers between devices with their start and end apart: 10, of which 9 were waited for; matrix products, arithmetic and copies ran while one was open for 8% of the time, Pallas kernels for 0%

commit v1 on v0

v1 whole, which is shorter than its diff:
```python
import functools

import jax
import jax.numpy as jnp
from jax import lax
from jax.experimental import pallas as pl
from jax.experimental.pallas import tpu as pltpu
from jax.sharding import Mesh
from jax.sharding import PartitionSpec as P

ROW = ("row_0", "row_1")
COL = ("col_0", "col_1")
COL_ROW = ("col_0", "col_1", "row_0", "row_1")
LOG2E = 1.4426950408889634
MIB = 1024 * 1024
F32 = jnp.float32
BF16 = jnp.bfloat16
HIGH = lax.Precision.HIGHEST


def call(body, outs, *args, scratch=(), limit=16, name=None):
    return pl.pallas_call(
        body,
        out_shape=outs,
        scratch_shapes=list(scratch),
        compiler_params=pltpu.CompilerParams(vmem_limit_bytes=limit * MIB),
        name=name,
    )(*args)


def shape(*dims, dtype=F32):
    return jax.ShapeDtypeStruct(dims, dtype)


def exchanged(pieces, axes):
    return lax.all_to_all(pieces, axes, 0, 0, tiled=True)


def from_everyone(value, axes):
    copies = lax.axis_size(axes)
    return exchanged(jnp.broadcast_to(value[None], (copies, *value.shape)), axes)


def split3(value):
    first = value.astype(BF16)
    rest = value - first.astype(F32)
    second = rest.astype(BF16)
    third = (rest - second.astype(F32)).astype(BF16)
    return first, second, third


def features_body(points_ref, scale_ref, out_ref):
    y = points_ref[...] * scale_ref[...]
    rows = y.shape[0]
    norm = -0.5 * jnp.sum(y * y, axis=1, keepdims=True)
    first, second, third = split3(y)
    n1, n2, n3 = (part.astype(F32) for part in split3(norm))
    lane = lax.broadcasted_iota(jnp.int32, (rows, 64), 1)
    zero = jnp.zeros((rows, 64), F32)
    norms = zero
    for at, part in ((0, n1), (1, n2), (2, n3), (3, n1), (4, n2), (5, n3)):
        norms = jnp.where(lane == at, part, norms)
    out_ref[:, :128] = jnp.concatenate([first.astype(F32), second.astype(F32)], axis=1).astype(BF16)
    out_ref[:, 128:] = jnp.concatenate([third.astype(F32), norms], axis=1).astype(BF16)


def kernel_body(left_ref, right_ref, test_ref, kern_ref, sketch_ref, right_scr, *, chunk):
    lane = lax.broadcasted_iota(jnp.int32, (1, 128), 1)

    def mask(test):
        return jnp.where(test, 1.0, 0.0).astype(BF16)

    low = mask(lane < 64)
    left_norm = mask((lane >= 64) & (lane < 67))
    right_norm = mask((lane >= 67) & (lane < 70))

    @pl.when(pl.program_id(0) == 0)
    def _():
        m1 = right_ref[:, :128]
        m2 = right_ref[:, 128:256]
        right_scr[:, 0:128] = m1
        right_scr[:, 128:256] = pltpu.roll(m1.astype(F32), 64, 1).astype(BF16)
        right_scr[:, 256:384] = m2 * (low + right_norm) + left_norm
        right_scr[:, 384:512] = m1 * low

    m1 = left_ref[:, :128]
    m2 = left_ref[:, 128:256]
    left = jnp.concatenate(
        [m1, m1, m1 * low + m2 * left_norm + right_norm, m2 * low], axis=1
    )
    total = None
    for start in range(0, right_ref.shape[0], chunk):
        exponent = lax.dot_general(
            left,
            right_scr[start : start + chunk, :],
            (((1,), (1,)), ((), ())),
            preferred_element_type=F32,
        )
        weights = jnp.exp2(exponent)
        kern_ref[:, start : start + chunk] = weights
        part = jnp.dot(
            weights.astype(BF16), test_ref[start : start + chunk, :], preferred_element_type=F32
        )
        total = part if total is None else total + part
    sketch_ref[...] = total


def kernel_and_sketch(left, right, test, tile=512, chunk=512):
    rows, columns, rank = left.shape[0], right.shape[0], test.shape[1]
    return pl.pallas_call(
        functools.partial(kernel_body, chunk=chunk),
        grid=(rows // tile,),
        in_specs=[
            pl.BlockSpec((tile, 256), lambda i: (i, 0)),
            pl.BlockSpec((columns, 256), lambda i: (0, 0)),
            pl.BlockSpec((columns, rank), lambda i: (0, 0)),
        ],
        out_specs=[
            pl.BlockSpec((tile, columns), lambda i: (i, 0)),
            pl.BlockSpec((tile, rank), lambda i: (i, 0)),
        ],
        out_shape=[shape(rows, columns), shape(rows, rank)],
        scratch_shapes=[pltpu.VMEM((columns, 512), BF16)],
        compiler_params=pltpu.CompilerParams(vmem_limit_bytes=48 * MIB),
        name="kernel_and_sketch",
    )(left, right, test)


def core_body(parts_ref, test_ref, targets_ref, ridge_ref, sketch_ref, out_ref):
    sketch = parts_ref[0]
    for i in range(1, parts_ref.shape[0]):
        sketch = sketch + parts_ref[i]
    sketch_ref[...] = sketch
    shifted = ridge_ref[0, 0] * test_ref[...].astype(F32) + sketch
    core = lax.dot_general(
        shifted, sketch, (((0,), (0,)), ((), ())), precision=HIGH, preferred_element_type=F32
    )
    targets = jnp.broadcast_to(targets_ref[...], (8, 256))
    projected = jnp.dot(targets, sketch, precision=HIGH, preferred_element_type=F32)
    square = jnp.sum(targets[0:1] * targets[0:1], axis=1, keepdims=True)
    row = lax.broadcasted_iota(jnp.int32, (8, 256), 0)
    extra = jnp.where(row == 0, projected, jnp.where(row == 1, square, 0.0))
    out_ref[:, 0:256] = core[0:128]
    out_ref[:, 256:512] = core[128:256]
    out_ref[:, 512:768] = jnp.zeros((128, 256), F32)
    out_ref[0:8, 512:768] = extra


def summed_body(parts_ref, out_ref):
    out_ref[...] = jnp.broadcast_to(jnp.sum(parts_ref[...], axis=0, keepdims=True), out_ref.shape)


def inverted(work_ref):
    size = work_ref.shape[0]
    sub = lax.broadcasted_iota(jnp.int32, (8, 1), 0)
    lanes = lax.broadcasted_iota(jnp.int32, (1, size), 1)
    for half in range(size // 128):
        window = slice(half * 128, half * 128 + 128)

        def panel_step(step, carry, half=half, window=window):
            at = half * 128 + step * 8
            columns = work_ref[:, window]
            panel = work_ref[pl.ds(at, 8), :]
            inner = panel[:, window]
            pick = [jnp.full((8, 128), 0, jnp.int32) + (step * 8 + j) for j in range(8)]
            diag = [jnp.take_along_axis(inner, pick[j], axis=1) for j in range(8)]
            for j in range(8):
                inverse = 1.0 / diag[j][j : j + 1, :]
                panel = jnp.where(lanes == at + j, jnp.where(sub == j, 1.0, 0.0), panel)
                wide = jnp.concatenate([inverse] * (size // 128), axis=1)
                row = panel[j : j + 1, :] * wide
                factor = jnp.concatenate([diag[j]] * (size // 128), axis=1)
                panel = jnp.where(sub == j, row, panel - factor * row)
                for k in range(j + 1, 8):
                    pivot_row = diag[k][j : j + 1, :] * inverse
                    diag[k] = jnp.where(sub == j, pivot_row, diag[k] - diag[j] * pivot_row)
            inside = (lanes >= at) & (lanes < at + 8)
            for group in range(size // 8):
                block = jnp.where(inside, 0.0, work_ref[group * 8 : group * 8 + 8, :])
                rows = columns[group * 8 : group * 8 + 8, :]
                for j in range(8):
                    factor = jnp.take_along_axis(rows, pick[j], axis=1)
                    factor = jnp.concatenate([factor] * (size // 128), axis=1)
                    block = block - factor * panel[j : j + 1, :]
                work_ref[group * 8 : group * 8 + 8, :] = block
            work_ref[pl.ds(at, 8), :] = panel
            return carry

        lax.fori_loop(0, 16, panel_step, 0)


def eight(row):
    return jnp.broadcast_to(row, (8, row.shape[1]))


def row_dot(a, b):
    return jnp.sum(a * b, axis=1, keepdims=True)


def times(vector, matrix, transposed=False):
    dims = (((1,), (1 if transposed else 0,)), ((), ()))
    return lax.dot_general(vector, matrix, dims, precision=HIGH, preferred_element_type=F32)


def first_body(packed_ref, sketch_ref, targets_ref, ridge_ref, inverse_ref, state_ref, send_ref):
    inverse_ref[0:128, :] = packed_ref[:, 0:256]
    inverse_ref[128:256, :] = packed_ref[:, 256:512]
    inverted(inverse_ref)
    projected = packed_ref[0:1, 512:768]
    square = packed_ref[1:2, 512:768]
    solved = times(eight(projected), inverse_ref[...])
    fitted = times(solved, sketch_ref[...], transposed=True)
    ridge = ridge_ref[0, 0]
    direction = (targets_ref[...] - fitted[0:1]) / ridge
    descent = (square - row_dot(projected, solved[0:1])) / ridge
    state_ref[0:1, :] = direction
    state_ref[1:2, :] = projected
    state_ref[2:3, :] = square
    state_ref[3:4, :] = descent
    send_ref[...] = jnp.broadcast_to(direction, send_ref.shape)


def product_body(kern_ref, vector_ref, out_ref):
    rows, columns = kern_ref.shape
    pieces = []
    for at in range(0, columns, 256):
        pieces.append(vector_ref[at // 256 : at // 256 + 1, :])
    vector = jnp.concatenate(pieces, axis=1)
    sub = lax.broadcasted_iota(jnp.int32, (8, 128), 0)
    lane = lax.broadcasted_iota(jnp.int32, (8, 128), 1)
    for base in range(0, rows, 128):
        packed = jnp.zeros((8, 128), F32)
        for group in range(16):
            at = base + group * 8
            block = kern_ref[at : at + 8, :] * vector
            acc = [block[:, k * 128 : k * 128 + 128] for k in range(columns // 128)]
            while len(acc) > 1:
                acc = [a + b for a, b in zip(acc[::2], acc[1::2])]
            column = jnp.sum(acc[0], axis=1, keepdims=True)
            packed = packed + jnp.where(lane == sub + group * 8, column, 0.0)
        out_ref[pl.program_id(0), :, base : base + 128] = eight(
            jnp.sum(packed, axis=0, keepdims=True)
        )


def kernel_times(kern, vector, tile=256):
    rows, columns = kern.shape
    out = pl.pallas_call(
        product_body,
        grid=(rows // tile,),
        in_specs=[
            pl.BlockSpec((tile, columns), lambda i: (i, 0)),
            pl.BlockSpec((columns // 256, 256), lambda i: (0, 0)),
        ],
        out_specs=pl.BlockSpec((rows // tile, 8, tile), lambda i: (0, 0, 0)),
        out_shape=shape(rows // tile, 8, tile),
        compiler_params=pltpu.CompilerParams(vmem_limit_bytes=24 * MIB),
        name="kernel_times",
    )(kern, vector)
    return out


def image_body(parts_ref, state_ref, sketch_ref, targets_ref, ridge_ref, image_ref, send_ref):
    image = jnp.sum(parts_ref[...], axis=0)[0:1] + ridge_ref[0, 0] * state_ref[0:1, :]
    image_ref[...] = eight(image)
    along = times(eight(image), sketch_ref[...])[0:1]
    lane = lax.broadcasted_iota(jnp.int32, (1, 128), 1)
    sums = jnp.where(
        lane == 0,
        row_dot(state_ref[0:1, :], image),
        jnp.where(
            lane == 1, row_dot(image, image), jnp.where(lane == 2, row_dot(targets_ref[...], image), 0.0)
        ),
    )
    send_ref[:, 0:256] = jnp.broadcast_to(along, (send_ref.shape[0], 256))
    send_ref[:, 256:384] = jnp.broadcast_to(sums, (send_ref.shape[0], 128))


def second_body(
    parts_ref, state_ref, image_ref, inverse_ref, sketch_ref, targets_ref, ridge_ref, next_ref, send_ref
):
    sums = jnp.sum(parts_ref[...], axis=0, keepdims=True)
    along = sums[:, 0:256]
    curve, image_square, cross = sums[:, 256:257], sums[:, 257:258], sums[:, 258:259]
    ridge = ridge_ref[0, 0]
    descent = state_ref[3:4, :]
    step = descent / curve
    projected = state_ref[1:2, :] - step * along
    solved = times(eight(projected), inverse_ref[...])
    fitted = times(solved, sketch_ref[...], transposed=True)[0:1]
    resid = targets_ref[...] - step * image_ref[0:1, :]
    square = state_ref[2:3, :] - 2.0 * step * cross + step * step * image_square
    fresh = (square - row_dot(projected, solved[0:1])) / ridge
    direction = (resid - fitted) / ridge + fresh / descent * state_ref[0:1, :]
    next_ref[0:1, :] = direction
    next_ref[1:2, :] = step
    next_ref[2:3, :] = fresh
    send_ref[...] = jnp.broadcast_to(direction, send_ref.shape)


def last_image_body(parts_ref, next_ref, ridge_ref, image_ref, send_ref):
    image = jnp.sum(parts_ref[...], axis=0)[0:1] + ridge_ref[0, 0] * next_ref[0:1, :]
    image_ref[...] = eight(image)
    send_ref[...] = jnp.broadcast_to(row_dot(next_ref[0:1, :], image), send_ref.shape)


def finish_body(
    parts_ref, state_ref, next_ref, image_ref, last_ref, targets_ref, coefficients_ref, residual_ref
):
    curve = jnp.sum(parts_ref[...], axis=0, keepdims=True)[:, 0:1]
    step = next_ref[1:2, :]
    last_step = next_ref[2:3, :] / curve
    coefficients_ref[...] = step * state_ref[0:1, :] + last_step * next_ref[0:1, :]
    residual_ref[...] = targets_ref[...] - step * image_ref[0:1, :] - last_step * last_ref[0:1, :]


def local(points, feature_scale, test_matrix, targets, ridge):
    everyone = lax.axis_size(COL_ROW)
    row_devices = lax.axis_size(ROW)
    own, rank = test_matrix.shape
    ridge = ridge.reshape(1, 1)
    targets = targets.reshape(1, own)
    scale = (feature_scale * LOG2E**0.5).reshape(1, -1)
    features = call(
        features_body, shape(own, 256, dtype=BF16), points, scale, name="features"
    )
    left = from_everyone(features, COL).reshape(-1, 256)
    right = from_everyone(features, ROW).reshape(-1, 256)
    test = from_everyone(test_matrix, ROW).reshape(-1, rank)
    kern, sketch_parts = kernel_and_sketch(left, right, test)
    sketch_parts = exchanged(sketch_parts.reshape(-1, own, rank), COL)
    sketch, packed = call(
        core_body,
        [shape(own, rank), shape(everyone, 768)],
        sketch_parts,
        test_matrix,
        targets,
        ridge,
        name="core",
    )
    packed = exchanged(packed, COL_ROW)
    packed = call(summed_body, shape(everyone, 768), packed, name="summed")
    packed = exchanged(packed, COL_ROW)
    inverse, state, send = call(
        first_body,
        [shape(rank, rank), shape(8, own), shape(row_devices, own)],
        packed,
        sketch,
        targets,
        ridge,
        name="first",
    )
    product = kernel_times(kern, exchanged(send, ROW))
    image, send = call(
        image_body,
        [shape(8, own), shape(everyone, 384)],
        exchanged(product, COL),
        state,
        sketch,
        targets,
        ridge,
        name="image",
    )
    following, send = call(
        second_body,
        [shape(8, own), shape(row_devices, own)],
        exchanged(send, COL_ROW),
        state,
        image,
        inverse,
        sketch,
        targets,
        ridge,
        name="second",
    )
    product = kernel_times(kern, exchanged(send, ROW))
    last, send = call(
        last_image_body,
        [shape(8, own), shape(everyone, 128)],
        exchanged(product, COL),
        following,
        ridge,
        name="last_image",
    )
    coefficients, residual = call(
        finish_body,
        [shape(1, own), shape(1, own)],
        exchanged(send, COL_ROW),
        state,
        following,
        image,
        last,
        targets,
        name="finish",
    )
    return coefficients.reshape(own), residual.reshape(own), sketch


def solution(mesh):
    split = Mesh(mesh.devices.reshape(4, 4, 4, 2), ROW + COL)
    return jax.shard_map(
        local,
        mesh=split,
        in_specs=(P(COL_ROW, None), P(), P(COL_ROW, None), P(COL_ROW), P()),
        out_specs=(P(COL_ROW), P(COL_ROW), P(COL_ROW, None)),
        check_vma=False,
    )
```

time: 488 us -> 297 us (0.61); the launches traced: 480 us -> 296 us
  matrix products: 149 us -> 0 us
  blocking collectives: 96.1 us -> 184 us
  Pallas kernels: 0 us -> 74.5 us
  waiting for transfers between devices: 91.8 us -> 25.6 us
  other arithmetic: 63.9 us -> 0.66 us
  starting transfers between devices: 54.7 us -> 6.51 us
  local copies, waits for them, and re-layouts: 16.9 us -> 3.92 us
  between operations: 7.37 us -> 1.42 us
    dot_general x10 -> x0, matrix products: 146 us -> none  [the longest x3 95 us: operate(): jnp.dot(weights, column_vec, precision=lax.Precision.HIGHEST, preferred_e...]
    all_to_all x12 -> x11, blocking collectives: 96.1 us -> 184 us  [exchanged(): return lax.all_to_all(pieces, axes, 0, 0, tiled=True)]
    pallas_call x0 -> x11, Pallas kernels: none -> 74.5 us  [the longest x8 29.1 us: call(): pl.pallas_call(body, out_shape=outs, scratch_shapes=list(scratch), compil...]
    all_to_all x10 -> x1, waiting for transfers between devices: 91.8 us -> 25.6 us  [exchanged(): return lax.all_to_all(pieces, axes, 0, 0, tiled=True)]
    another operation x12 -> x0, other arithmetic: 53.9 us -> none  [the longest x6 34 us: local(): lower = jnp.linalg.cholesky(core)]
    all_to_all x10 -> x1, starting transfers between devices: 54.7 us -> 6.51 us  [exchanged(): return lax.all_to_all(pieces, axes, 0, 0, tiled=True)]
    broadcast_in_dim x16 -> x3, local copies, waits for them, and re-layouts: 9.58 us -> 0.46 us  [from_everyone(): jnp.broadcast_to(value[None], (copies, *value.shape))]
    reduce_sum x22 -> x0, other arithmetic: 6.95 us -> none  [the longest x8 2.79 us: taken_together(): return jnp.sum(everything, axis=0)]
  transfers between devices with their start and end apart: 10 -> 1, of which waited for: 9 -> 1; matrix products, arithmetic and copies ran while one was open for 8% -> 0% of each run, Pallas kernels for 0% -> 0%
where the time goes in v1:
time: 297 us; the launch traced here: 296 us
  blocking collectives  184 us (62%)
  Pallas kernels  74.5 us (25%)
  waiting for transfers between devices  25.6 us (9%)
  starting transfers between devices  6.51 us (2%)
  local copies, waits for them, and re-layouts  3.92 us (1%)
    all_to_all x11, blocking collectives, exchanged(): return lax.all_to_all(pieces, axes, 0, 0, tiled=True)  184 us
    pallas_call x8, Pallas kernels, call(): pl.pallas_call(body, out_shape=outs, scratch_shapes=list(scratch), compil...  29.1 us
    all_to_all x1, waiting for transfers between devices, exchanged(): return lax.all_to_all(pieces, axes, 0, 0, tiled=True)  25.6 us
    pallas_call x2, Pallas kernels, kernel_times(): pl.pallas_call(product_body, grid=(rows // tile,), in_specs=[pl.BlockSpec...  24.6 us
    pallas_call x1, Pallas kernels, kernel_and_sketch(): pl.pallas_call(functools.partial(kernel_body, chunk=chunk), grid=(rows //...  20.8 us
    all_to_all x1, starting transfers between devices, exchanged(): return lax.all_to_all(pieces, axes, 0, 0, tiled=True)  6.51 us
  transfers between devices with their start and end apart: 1, of which 1 were waited for; matrix products, arithmetic and copies ran while one was open for 0% of the time, Pallas kernels for 0%

profile of v1, /device:TPU:1, one launch (start us, length us, event | category | flops | bytes accessed | tf_op | source)
XLA Modules:
  0.0 296.4 jit_solution(9598121758254003080)
XLA Ops:
  0.6 0.9 copy.9.points_ref
  1.6 0.7 multiply_bitcast_fusion.scale_ref
  2.2 0.2 features.1
  2.5 0.1 broadcast_in_dim.6
  2.5 20.5 %all_to_all.96 = bf16[8,256,256]{2,1,0:T(8,128)(2,1)S(1)} all-to-all(bf16[8,256,256]{2,1,0:T(8,128)(2,1)S(1)} %broadcast_in_dim.6), channel_id=1, replica_groups=mesh['row_0'=4,'row_1'=4,'col_0'=4,'col_1'=2] {'col_0','col_1'}, dimensions={0} | all-to-all | bytes 2097152 | tf_op jit(solution)/shard_map/all_to_all | solution.py:36
  23.1 0.2 broadcast_in_dim.7
  23.3 34.5 %all_to_all.97 = bf16[16,256,256]{2,1,0:T(8,128)(2,1)S(1)} all-to-all(bf16[16,256,256]{2,1,0:T(8,128)(2,1)S(1)} %broadcast_in_dim.7), channel_id=1, replica_groups=mesh['row_0'=4,'row_1'=4,'col_0'=4,'col_1'=2] {'row_0','row_1'}, dimensions={0} | all-to-all | bytes 4194304 | tf_op jit(solution)/shard_map/all_to_all | solution.py:36
  57.7 0.2 broadcast_in_dim.8
  57.9 29.9 %all_to_all.98 = bf16[16,256,256]{2,1,0:T(8,128)(2,1)} all-to-all(bf16[16,256,256]{2,1,0:T(8,128)(2,1)S(1)} %broadcast_in_dim.8), channel_id=1, replica_groups=mesh['row_0'=4,'row_1'=4,'col_0'=4,'col_1'=2] {'row_0','row_1'}, dimensions={0} | all-to-all | bytes 4194304 | tf_op jit(solution)/shard_map/all_to_all | solution.py:36
  87.9 20.8 %kernel_and_sketch.1 = (f32[2048,4096]{1,0:T(8,128)}, f32[2048,256]{1,0:T(8,128)S(1)}) custom-call(bf16[2048,256]{1,0:T(8,128)(2,1)S(1)} %bitcast.40, bf16[4096,256]{1,0:T(8,128)(2,1)S(1)} %bitcast.39, bf16[4096,256]{1,0:T(8,128)(2,1)} %bitcast.59), custom_call_target="tpu_custom_call" | custom-call | tf_op jit(solution)/shard_map/kernel_and_sketch/pallas_call | solution.py:110
  108.7 1.3 copy-done.1
  110.0 6.5 %all-to-all-start.3 = ((f32[8,256,256]{2,1,0:T(8,128)}), f32[8,256,256]{2,1,0:T(8,128)S(1)}, u32[]{:S(2)}, u32[]{:S(2)}) async-start(f32[8,256,256]{2,1,0:T(8,128)} %bitcast.41), calls=%async_computation.3 | async-start | bytes 4194304 | tf_op jit(solution)/shard_map/all_to_all | solution.py:36
  117.2 25.6 %all-to-all-done.3.parts_ref = f32[8,256,256]{2,1,0:T(8,128)S(1)} async-done(((f32[8,256,256]{2,1,0:T(8,128)}), f32[8,256,256]{2,1,0:T(8,128)S(1)}, u32[]{:S(2)}, u32[]{:S(2)}) %all-to-all-start.3) | async-done | bytes 2097184 | tf_op jit(solution)/shard_map/all_to_all | solution.py:36
  142.8 0.9 core.1
  143.6 0.4 copy.10
  144.0 17.2 %all_to_all.99 = f32[128,1,768]{2,1,0:T(1,128)S(1)} all-to-all(f32[128,1,768]{2,1,0:T(1,128)S(1)} %copy.10), channel_id=1, replica_groups=mesh['row_0'=4,'row_1'=4,'col_0'=4,'col_1'=2] {'col_0','col_1','row_0','..., dimensions={0} | all-to-all | bytes 786432 | tf_op jit(solution)/shard_map/all_to_all | solution.py:36
  161.4 0.4 copy.11
  161.8 16.5 %all_to_all.100 = f32[128,1,768]{2,1,0:T(1,128)S(1)} all-to-all(f32[128,1,768]{2,1,0:T(1,128)S(1)} %copy.11), channel_id=1, replica_groups=mesh['row_0'=4,'row_1'=4,'col_0'=4,'col_1'=2] {'col_0','col_1','row_0','..., dimensions={0} | all-to-all | bytes 786432 | tf_op jit(solution)/shard_map/all_to_all | solution.py:36
  178.4 26.2 %first.1 = (f32[256,256]{1,0:T(8,128)S(1)}, f32[8,256]{1,0:T(8,128)S(1)}, f32[16,256]{1,0:T(8,128)S(1)}) custom-call(f32[128,768]{1,0:T(8,128)S(1)} %bitcast.42, f32[256,256]{1,0:T(8,128)S(1)} %copy-done, f32[1,256]{1,0:T(1,128)S(1)} %bitcast.53, f32[1,1]{1,0:T(1,128)} %bitcast.35.ridge_ref), custom_call_target="tpu_custom_call" | custom-call | tf_op jit(solution)/shard_map/first/pallas_call | solution.py:22
  204.6 9.1 %all_to_all.101 = f32[16,1,256]{2,1,0:T(1,128)S(1)} all-to-all(f32[16,1,256]{2,1,0:T(1,128)S(1)} %copy.12), channel_id=1, replica_groups=mesh['row_0'=4,'row_1'=4,'col_0'=4,'col_1'=2] {'row_0','row_1'}, dimensions={0} | all-to-all | bytes 32768 | tf_op jit(solution)/shard_map/all_to_all | solution.py:36
  213.7 12.3 %kernel_times.2 = f32[8,8,256]{2,1,0:T(8,128)S(1)} custom-call(f32[2048,4096]{1,0:T(8,128)} %get-tuple-element.18.kern_ref, f32[16,256]{1,0:T(8,128)S(1)} %bitcast.49), custom_call_target="tpu_custom_call" | custom-call | tf_op jit(solution)/shard_map/kernel_times/pallas_call | solution.py:248
  226.0 9.5 %all_to_all.102.parts_ref = f32[8,8,256]{2,1,0:T(8,128)S(1)} all-to-all(f32[8,8,256]{2,1,0:T(8,128)S(1)} %kernel_times.2), channel_id=1, replica_groups=mesh['row_0'=4,'row_1'=4,'col_0'=4,'col_1'=2] {'col_0','col_1'}, dimensions={0} | all-to-all | bytes 131072 | tf_op jit(solution)/shard_map/all_to_all | solution.py:36
  235.5 0.2 image.1
  235.7 0.2 copy.13
  236.0 14.5 %all_to_all.103 = f32[128,1,384]{2,1,0:T(1,128)S(1)} all-to-all(f32[128,1,384]{2,1,0:T(1,128)S(1)} %copy.13), channel_id=1, replica_groups=mesh['row_0'=4,'row_1'=4,'col_0'=4,'col_1'=2] {'col_0','col_1','row_0','..., dimensions={0} | all-to-all | bytes 393216 | tf_op jit(solution)/shard_map/all_to_all | solution.py:36
  250.5 0.7 second.1
  251.3 9.1 %all_to_all.104 = f32[16,1,256]{2,1,0:T(1,128)S(1)} all-to-all(f32[16,1,256]{2,1,0:T(1,128)S(1)} %copy.14), channel_id=1, replica_groups=mesh['row_0'=4,'row_1'=4,'col_0'=4,'col_1'=2] {'row_0','row_1'}, dimensions={0} | all-to-all | bytes 32768 | tf_op jit(solution)/shard_map/all_to_all | solution.py:36
  260.4 12.3 %kernel_times.3 = f32[8,8,256]{2,1,0:T(8,128)S(1)} custom-call(f32[2048,4096]{1,0:T(8,128)} %get-tuple-element.18.kern_ref, f32[16,256]{1,0:T(8,128)S(1)} %bitcast.50), custom_call_target="tpu_custom_call" | custom-call | tf_op jit(solution)/shard_map/kernel_times/pallas_call | solution.py:248
  272.7 9.5 %all_to_all.105.parts_ref = f32[8,8,256]{2,1,0:T(8,128)S(1)} all-to-all(f32[8,8,256]{2,1,0:T(8,128)S(1)} %kernel_times.3), channel_id=1, replica_groups=mesh['row_0'=4,'row_1'=4,'col_0'=4,'col_1'=2] {'col_0','col_1'}, dimensions={0} | all-to-all | bytes 131072 | tf_op jit(solution)/shard_map/all_to_all | solution.py:36
  282.1 0.1 last_image.1
  282.3 13.5 %all_to_all.106 = f32[128,1,128]{2,1,0:T(1,128)S(1)} all-to-all(f32[128,1,128]{2,1,0:T(1,128)S(1)} %bitcast.51), channel_id=1, replica_groups=mesh['row_0'=4,'row_1'=4,'col_0'=4,'col_1'=2] {'col_0','col_1','row_0','..., dimensions={0} | all-to-all | bytes 131072 | tf_op jit(solution)/shard_map/all_to_all | solution.py:36
  295.8 0.7 finish.1
  (15 shorter events, 0.2 us)
Async XLA Ops:
  23.3 34.5 %copy-start.2 = (bf16[256,256]{1,0:T(8,128)(2,1)S(1)}, bf16[256,256]{1,0:T(8,128)(2,1)}, u32[]{:S(2)}) copy-start(bf16[256,256]{1,0:T(8,128)(2,1)} %test_ref.1) | copy-start | bytes 393220
  108.7 1.3 copy-start.1
  110.0 32.7 %copy-start.3 = (f32[256]{0:T(256)S(1)}, f32[256]{0:T(256)}, u32[]{:S(2)}) copy-start(f32[256]{0:T(256)} %param.8) | copy-start | bytes 3076
  110.0 32.7 %all-to-all-start.3 = ((f32[8,256,256]{2,1,0:T(8,128)}), f32[8,256,256]{2,1,0:T(8,128)S(1)}, u32[]{:S(2)}, u32[]{:S(2)}) async-start(f32[8,256,256]{2,1,0:T(8,128)} %bitcast.41), calls=%async_computation.3 | async-start | bytes 4194304 | tf_op jit(solution)/shard_map/all_to_all | solution.py:36
  161.3 17.1 %copy-start = (f32[256,256]{1,0:T(8,128)S(1)}, f32[256,256]{1,0:T(8,128)}, u32[]{:S(2)}) copy-start(f32[256,256]{1,0:T(8,128)} %get-tuple-element.17.sketch_ref) | copy-start | bytes 786436
